TPU v7x, 32 devices: a whole 2x2x4 slice. The times are simulated.
32 devices in a mesh: blk: 4 (over x, core), grp: 8 (over z, y).
Axes of the slice: x: 2, y: 2, z: 4, core: 2. Of those that a mesh axis runs over, the one named last changes fastest.
Arguments:
- text: bfloat16 [32, 512], P(('blk', 'grp')), may hold values from -20 to 20
- keys: bfloat16 [32, 196, 512], P(('blk', 'grp')), may hold values from -400 to 400
- values: bfloat16 [32, 196, 512], P(('blk', 'grp')), may hold values from -5 to 5
- pair_image: int32 [32], replicated, may hold values from 0 to 31, each once
Outputs:
- caption_loss: float32 [32], P(('blk', 'grp'))
- grad_text: float32 [32, 512], P(('blk', 'grp'))
- grad_keys: float32 [32, 196, 512], P(('blk', 'grp'))
- grad_values: float32 [32, 196, 512], P(('blk', 'grp'))
All inputs are finite; a program needn't handle non-finite values.
Results may differ from a plain program's by a relative error of at most 0.008.
Values may be sent and summed in bfloat16 or wider, within the bound.
A program may use at most 64 MiB of HBM per device.

v0:
```python
import jax
import jax.numpy as jnp
from jax import lax
from jax.sharding import PartitionSpec as P

HEADS = 8


EPS = 1e-06
LOGIT_SCALE = 10.0
LOGIT_BIAS = -1.0


def passed_along(block, axis, distance):
    devices = range(lax.axis_size(axis))
    route = [((i - distance) % len(devices), i) for i in devices]
    return lax.ppermute(block, axis, route)


def image_terms(block_text, normed, tnorm, pairs, image_id, keys_one, values_one):
    count = block_text.shape[0]
    width = block_text.shape[1]
    depth = width // HEADS
    queries = block_text.reshape(count, HEADS, depth)
    patch_keys = keys_one.reshape(-1, HEADS, depth)
    patch_values = values_one.reshape(-1, HEADS, depth)
    scores = jnp.einsum(
        "chd,phd->chp", queries, patch_keys, preferred_element_type=jnp.float32
    ) * depth ** (-0.5)
    weights = jax.nn.softmax(scores, axis=-1)
    attn = weights.astype(jnp.bfloat16)
    pooled = jnp.einsum(
        "chp,phd->chd", attn, patch_values, preferred_element_type=jnp.float32
    ).reshape(count, width)
    pnorm = lax.rsqrt(jnp.mean(pooled * pooled, -1, keepdims=True) + EPS)
    unit = pooled * pnorm
    cosine = jnp.mean(unit * normed, -1)
    logit = LOGIT_SCALE * cosine + LOGIT_BIAS
    label = jnp.where(pairs == image_id, 1.0, -1.0).astype(jnp.float32)
    loss = jax.nn.softplus(-label * logit)
    slope = -label * jax.nn.sigmoid(-label * logit)
    dcos = LOGIT_SCALE / width * slope[:, None]
    dunit = dcos * normed
    dnormed = dcos * unit
    dpool = pnorm * (dunit - unit * jnp.mean(dunit * unit, -1, keepdims=True))
    dout = dpool.astype(jnp.bfloat16).reshape(count, HEADS, depth)
    dattn = jnp.einsum("chd,phd->chp", dout, patch_values, preferred_element_type=jnp.float32)
    grad_v = jnp.einsum("chp,chd->phd", attn, dout, preferred_element_type=jnp.float32).reshape(
        -1, width
    )
    dscore = (
        weights * (dattn - jnp.sum(weights * dattn, -1, keepdims=True)) * depth ** (-0.5)
    ).astype(jnp.bfloat16)
    grad_q = jnp.einsum(
        "chp,phd->chd", dscore, patch_keys, preferred_element_type=jnp.float32
    ).reshape(count, width)
    grad_k = jnp.einsum(
        "chp,chd->phd", dscore, queries, preferred_element_type=jnp.float32
    ).reshape(-1, width)
    grad_x = grad_q + tnorm * (dnormed - normed * jnp.mean(dnormed * normed, -1, keepdims=True))
    return (loss, grad_x, grad_k, grad_v)


def pair_block(block_text, pair_image, first_caption, keys, values, first_image):
    count = block_text.shape[0]
    width = block_text.shape[1]
    text_wide = block_text.astype(jnp.float32)
    tnorm = lax.rsqrt(jnp.mean(text_wide * text_wide, -1, keepdims=True) + EPS)
    normed = text_wide * tnorm
    pairs = lax.dynamic_slice_in_dim(pair_image, first_caption, count)
    image_ids = first_image + jnp.arange(keys.shape[0], dtype=jnp.int32)

    def one_image(carry, item):
        keys_one, values_one, image_id = item
        loss, grad_x, grad_k, grad_v = image_terms(
            block_text, normed, tnorm, pairs, image_id, keys_one, values_one
        )
        return ((carry[0] + loss, carry[1] + grad_x), (grad_k, grad_v))

    start = (jnp.zeros((count,), jnp.float32), jnp.zeros((count, width), jnp.float32))
    (loss_sum, grad_text), (grad_keys, grad_values) = lax.scan(
        one_image, start, (keys, values, image_ids)
    )
    return (loss_sum, grad_text, grad_keys, grad_values)


def local(text, keys, values, pair_image):
    per_device = keys.shape[0]
    groups = lax.axis_size("blk")
    members = lax.axis_size("grp")
    group_index = lax.axis_index("blk")
    first_image = (group_index * members + lax.axis_index("grp")) * per_device
    image_total = per_device * groups * members
    group_text = lax.all_gather(text, "grp", axis=0, tiled=True)
    span = group_text.shape[0]
    carried = (jnp.zeros((span,), jnp.float32), jnp.zeros((span, text.shape[1]), jnp.float32))
    grad_keys = jnp.zeros(keys.shape, jnp.float32)
    grad_values = jnp.zeros(values.shape, jnp.float32)
    for turn in range(groups):
        source = (group_index - turn) % groups
        loss_part, grad_part, keys_part, values_part = pair_block(
            group_text, pair_image, source * span, keys, values, first_image
        )
        carried = (carried[0] + loss_part, carried[1] + grad_part)
        grad_keys = grad_keys + keys_part
        grad_values = grad_values + values_part
        if turn + 1 < groups:
            group_text = passed_along(group_text, "blk", 1)
        carried = passed_along((carried[0], carried[1]), "blk", 1)
    loss_own, grad_own = (
        lax.psum_scatter(carried[0], "grp", scatter_dimension=0, tiled=True),
        lax.psum_scatter(carried[1], "grp", scatter_dimension=0, tiled=True),
    )
    return (loss_own / image_total, grad_own, grad_keys, grad_values)


def solution(mesh):
    placed = (
        P(("blk", "grp"), None),
        P(("blk", "grp"), None, None),
        P(("blk", "grp"), None, None),
        P(),
    )
    return jax.shard_map(
        local,
        mesh=mesh,
        in_specs=placed,
        out_specs=(
            P(("blk", "grp")),
            P(("blk", "grp"), None),
            P(("blk", "grp"), None, None),
            P(("blk", "grp"), None, None),
        ),
        check_vma=False,
    )
```

profile of v0, /device:TPU:0, one launch (start us, length us, event | category | flops | bytes accessed | tf_op | source)
XLA Modules:
  0.0 104.7 jit_solution(5783523239401266928)
XLA Ops:
  0.6 28.1 %all-gather = bf16[8,1,512]{2,1,0:T(2,128)(2,1)S(1)} all-gather(bf16[1,1,512]{2,1,0:T(2,128)(2,1)} %bitcast.91), channel_id=1, replica_groups=mesh['blk'=4,'grp'=8] {'grp'}, dimensions={0}, use_global_device_ids=true | all-gather | bytes 9216 | tf_op jit(solution)/shard_map/all_gather | solution.py:94
  28.9 1.1 %copy.92 = bf16[1,196,512]{1,2,0:T(8,128)(2,1)S(1)} copy(bf16[1,196,512]{2,1,0:T(8,128)(2,1)} %param.6) | data formatting | bytes 401408 | tf_op args[2]
  30.4 1.3 %fusion.180 = (f32[8,8]{0,1:T(8,128)S(1)}, f32[8,8,196]{2,0,1:T(8,128)S(1)}) fusion(f32[8,8,196]{2,0,1:T(8,128)S(1)} %fusion.31), kind=kOutput, calls=%fused_computation.247 | output fusion | flops 25283 | bytes 100608 | tf_op jit(solution)/shard_map/while/body/eval_jaxpr/sub | solution.py:30
  31.8 0.4 multiply_reduce_fusion.7
  32.3 0.2 fusion.97
  32.5 0.5 copy-done.1
  33.0 1.6 %collective-permute-start = (f32[8]{0:T(128)S(1)}, f32[8]{0:T(128)S(1)}, u32[]{:S(2)}, u32[]{:S(2)}) collective-permute-start(f32[8]{0:T(128)S(1)} %compare_select_fusion.3), channel_id=1, source_target_pairs={{24,0},{0,8},{8,16},{16,24},{25,1},{1,9},{9,17},{17,25},{26,2},{2,... | collective-permute-start | bytes 104 | tf_op jit(solution)/shard_map/ppermute | solution.py:17
  34.7 0.2 fusion.98
  35.2 0.3 convolution_bitcast_fusion.7
  35.7 0.4 fusion.36
  36.1 0.3 fusion.130
  36.6 0.6 copy-done.2
  37.2 0.6 dynamic-slice
  37.9 0.1 fusion.30
  38.0 1.3 %fusion.179 = (f32[8,8]{0,1:T(8,128)S(1)}, f32[8,8,196]{2,0,1:T(8,128)S(1)}) fusion(f32[8,8,196]{2,0,1:T(8,128)S(1)} %fusion.30), kind=kOutput, calls=%fused_computation.246 | output fusion | flops 25283 | bytes 100608 | tf_op jit(solution)/shard_map/while/body/eval_jaxpr/sub | solution.py:30
  39.3 0.4 multiply_reduce_fusion.6
  40.0 0.2 fusion.103
  40.3 0.7 collective-permute-start.2
  40.9 0.2 fusion.104
  41.5 0.3 convolution_bitcast_fusion.6
  41.8 0.4 convolution_add_fusion.5
  42.2 0.3 convolution_add_fusion.2
  42.7 3.0 %collective-permute-done.3 = bf16[8,512]{1,0:T(8,128)(2,1)S(1)} collective-permute-done((bf16[8,512]{1,0:T(8,128)(2,1)S(1)}, bf16[8,512]{1,0:T(8,128)(2,1)S(1)}, u32[]{:S(2)}, u32[]{:S(2)}) %collective-permute-start.3) | collective-permute-done | bytes 8224 | tf_op jit(solution)/shard_map/ppermute | solution.py:17
  45.8 0.1 fusion.29
  45.9 1.3 %fusion.178 = (f32[8,8]{0,1:T(8,128)S(1)}, f32[8,8,196]{2,0,1:T(8,128)S(1)}) fusion(f32[8,8,196]{2,0,1:T(8,128)S(1)} %fusion.29), kind=kOutput, calls=%fused_computation.245 | output fusion | flops 25283 | bytes 100608 | tf_op jit(solution)/shard_map/while/body/eval_jaxpr/sub | solution.py:30
  47.2 0.4 multiply_reduce_fusion.5
  47.9 0.2 fusion.110
  48.3 1.6 %collective-permute-start.8 = (f32[8,512]{1,0:T(8,128)S(1)}, f32[8,512]{1,0:T(8,128)S(1)}, u32[]{:S(2)}, u32[]{:S(2)}) collective-permute-start(f32[8,512]{1,0:T(8,128)S(1)} %fusion.108), channel_id=1, source_target_pairs={{24,0},{0,8},{8,16},{16,24},{25,1},{1,9},{9,17},{17,25},{26,2},{2,... | collective-permute-start | bytes 49160 | tf_op jit(solution)/shard_map/ppermute | solution.py:17
  49.9 0.2 fusion.111
  50.4 0.3 convolution_bitcast_fusion.5
  50.7 0.4 convolution_add_fusion.4
  51.2 0.3 convolution_add_fusion.1
  51.7 3.0 %collective-permute-done.5 = bf16[8,512]{1,0:T(8,128)(2,1)S(1)} collective-permute-done((bf16[8,512]{1,0:T(8,128)(2,1)S(1)}, bf16[8,512]{1,0:T(8,128)(2,1)S(1)}, u32[]{:S(2)}, u32[]{:S(2)}) %collective-permute-start.5) | collective-permute-done | bytes 8224 | tf_op jit(solution)/shard_map/ppermute | solution.py:17
  54.9 1.3 %fusion.177 = (f32[8,8]{0,1:T(8,128)S(1)}, f32[8,8,196]{2,0,1:T(8,128)S(1)}) fusion(f32[8,8,196]{2,0,1:T(8,128)S(1)} %fusion.28), kind=kOutput, calls=%fused_computation.244 | output fusion | flops 25283 | bytes 100608 | tf_op jit(solution)/shard_map/while/body/eval_jaxpr/sub | solution.py:30
  56.2 0.4 multiply_reduce_fusion.4
  56.8 0.2 fusion.117
  57.2 0.2 fusion.118
  57.7 0.4 convolution_add_fusion.3
  58.1 0.3 convolution_bitcast_fusion.4
  58.5 0.6 collective-permute-start.9
  59.3 2.4 %collective-permute-done.9 = f32[8,512]{1,0:T(8,128)S(1)} collective-permute-done((f32[8,512]{1,0:T(8,128)S(1)}, f32[8,512]{1,0:T(8,128)S(1)}, u32[]{:S(2)}, u32[]{:S(2)}) %collective-permute-start.9) | collective-permute-done | bytes 16416 | tf_op jit(solution)/shard_map/ppermute | solution.py:17
  61.8 0.3 convolution_add_fusion
  62.1 1.0 copy.116
  63.2 1.0 copy.117
  64.2 0.8 collective-permute-done.10
  65.0 35.4 %all-reduce.2 = (f32[8]{0:T(128)S(1)}, f32[8,512]{1,0:T(8,128)S(1)}) all-reduce(f32[8]{0:T(128)S(1)} %collective-permute-done.6, f32[8,512]{1,0:T(8,128)S(1)} %collective-permute-done.10), channel_id=2, replica_groups=mesh['blk'=4,'grp'=8] {'grp'}, use_global_device_ids=true, to_apply=%region_20.21.clone | all-reduce | flops 4104 | bytes 32832
  100.4 1.3 %dynamic-slice.1 = f32[1]{0:T(128)} dynamic-slice(f32[8]{0:T(128)S(1)} %get-tuple-element.148, u32[]{:T(128)} %bitcast.23), dynamic_slice_sizes={1} | dynamic-slice | bytes 12
  101.7 1.2 %constant_dynamic-slice_fusion = f32[1,512]{1,0:T(1,128)} fusion(f32[8,512]{1,0:T(8,128)S(1)} %get-tuple-element.149, u32[]{:T(128)} %bitcast.23), kind=kLoop, calls=%fused_computation.211 | loop fusion | bytes 4100
  (81 shorter events, 4.4 us)
Async XLA Ops:
  28.8 9.0 %collective-permute-start.1 = (bf16[8,512]{1,0:T(8,128)(2,1)S(1)}, bf16[8,512]{1,0:T(8,128)(2,1)S(1)}, u32[]{:S(2)}, u32[]{:S(2)}) collective-permute-start(bf16[8,512]{1,0:T(8,128)(2,1)S(1)} %get-tuple-element.153), channel_id=1, source_target_pairs={{24,0},{0,8},{8,16},{16,24},{25,1},{1,9},{9,17},{17,25},{26,2},{2,... | collective-permute-start | bytes 24584 | tf_op jit(solution)/shard_map/ppermute | solution.py:17
  28.9 1.1 %copy-start = (bf16[1,196,512]{2,1,0:T(8,128)(2,1)S(1)}, bf16[1,196,512]{2,1,0:T(8,128)(2,1)}, u32[]{:S(2)}) copy-start(bf16[1,196,512]{2,1,0:T(8,128)(2,1)} %param.5) | copy-start | bytes 602116
  32.3 0.7 copy-start.1
  33.0 7.1 %collective-permute-start = (f32[8]{0:T(128)S(1)}, f32[8]{0:T(128)S(1)}, u32[]{:S(2)}, u32[]{:S(2)}) collective-permute-start(f32[8]{0:T(128)S(1)} %compare_select_fusion.3), channel_id=1, source_target_pairs={{24,0},{0,8},{8,16},{16,24},{25,1},{1,9},{9,17},{17,25},{26,2},{2,... | collective-permute-start | bytes 104 | tf_op jit(solution)/shard_map/ppermute | solution.py:17
  35.7 12.5 %collective-permute-start.7 = (f32[8,512]{1,0:T(8,128)S(1)}, f32[8,512]{1,0:T(8,128)S(1)}, u32[]{:S(2)}, u32[]{:S(2)}) collective-permute-start(f32[8,512]{1,0:T(8,128)S(1)} %fusion.101), channel_id=1, source_target_pairs={{24,0},{0,8},{8,16},{16,24},{25,1},{1,9},{9,17},{17,25},{26,2},{2,... | collective-permute-start | bytes 49160 | tf_op jit(solution)/shard_map/ppermute | solution.py:17
  36.6 0.7 copy-start.2
  40.3 7.8 %collective-permute-start.2 = (f32[8]{0:T(128)S(1)}, f32[8]{0:T(128)S(1)}, u32[]{:S(2)}, u32[]{:S(2)}) collective-permute-start(f32[8]{0:T(128)S(1)} %get-tuple-element.171), channel_id=1, source_target_pairs={{24,0},{0,8},{8,16},{16,24},{25,1},{1,9},{9,17},{17,25},{26,2},{2,... | collective-permute-start | bytes 104 | tf_op jit(solution)/shard_map/ppermute | solution.py:17
  42.6 3.1 %collective-permute-start.3 = (bf16[8,512]{1,0:T(8,128)(2,1)S(1)}, bf16[8,512]{1,0:T(8,128)(2,1)S(1)}, u32[]{:S(2)}, u32[]{:S(2)}) collective-permute-start(bf16[8,512]{1,0:T(8,128)(2,1)S(1)} %collective-permute-done.1), channel_id=1, source_target_pairs={{24,0},{0,8},{8,16},{16,24},{25,1},{1,9},{9,17},{17,25},{26,2},{2,... | collective-permute-start | bytes 24584 | tf_op jit(solution)/shard_map/ppermute | solution.py:17
  48.2 8.9 %collective-permute-start.4 = (f32[8]{0:T(128)S(1)}, f32[8]{0:T(128)S(1)}, u32[]{:S(2)}, u32[]{:S(2)}) collective-permute-start(f32[8]{0:T(128)S(1)} %get-tuple-element.169), channel_id=1, source_target_pairs={{24,0},{0,8},{8,16},{16,24},{25,1},{1,9},{9,17},{17,25},{26,2},{2,... | collective-permute-start | bytes 104 | tf_op jit(solution)/shard_map/ppermute | solution.py:17
  48.3 10.1 %collective-permute-start.8 = (f32[8,512]{1,0:T(8,128)S(1)}, f32[8,512]{1,0:T(8,128)S(1)}, u32[]{:S(2)}, u32[]{:S(2)}) collective-permute-start(f32[8,512]{1,0:T(8,128)S(1)} %fusion.108), channel_id=1, source_target_pairs={{24,0},{0,8},{8,16},{16,24},{25,1},{1,9},{9,17},{17,25},{26,2},{2,... | collective-permute-start | bytes 49160 | tf_op jit(solution)/shard_map/ppermute | solution.py:17
  51.5 3.1 %collective-permute-start.5 = (bf16[8,512]{1,0:T(8,128)(2,1)S(1)}, bf16[8,512]{1,0:T(8,128)(2,1)S(1)}, u32[]{:S(2)}, u32[]{:S(2)}) collective-permute-start(bf16[8,512]{1,0:T(8,128)(2,1)S(1)} %collective-permute-done.3), channel_id=1, source_target_pairs={{24,0},{0,8},{8,16},{16,24},{25,1},{1,9},{9,17},{17,25},{26,2},{2,... | collective-permute-start | bytes 24584 | tf_op jit(solution)/shard_map/ppermute | solution.py:17
  57.1 7.0 %collective-permute-start.6 = (f32[8]{0:T(128)S(1)}, f32[8]{0:T(128)S(1)}, u32[]{:S(2)}, u32[]{:S(2)}) collective-permute-start(f32[8]{0:T(128)S(1)} %get-tuple-element.155), channel_id=1, source_target_pairs={{24,0},{0,8},{8,16},{16,24},{25,1},{1,9},{9,17},{17,25},{26,2},{2,... | collective-permute-start | bytes 104 | tf_op jit(solution)/shard_map/ppermute | solution.py:17
  58.5 3.2 %collective-permute-start.9 = (f32[8,512]{1,0:T(8,128)S(1)}, f32[8,512]{1,0:T(8,128)S(1)}, u32[]{:S(2)}, u32[]{:S(2)}) collective-permute-start(f32[8,512]{1,0:T(8,128)S(1)} %fusion.115), channel_id=1, source_target_pairs={{24,0},{0,8},{8,16},{16,24},{25,1},{1,9},{9,17},{17,25},{26,2},{2,... | collective-permute-start | bytes 49160 | tf_op jit(solution)/shard_map/ppermute | solution.py:17
  61.8 3.2 %collective-permute-start.10 = (f32[8,512]{1,0:T(8,128)S(1)}, f32[8,512]{1,0:T(8,128)S(1)}, u32[]{:S(2)}, u32[]{:S(2)}) collective-permute-start(f32[8,512]{1,0:T(8,128)S(1)} %fusion.122), channel_id=1, source_target_pairs={{24,0},{0,8},{8,16},{16,24},{25,1},{1,9},{9,17},{17,25},{26,2},{2,... | collective-permute-start | bytes 49160 | tf_op jit(solution)/shard_map/ppermute | solution.py:17
where the time goes:
time: 105 us
  blocking collectives  63.5 us (60%)
  waiting for transfers between devices  9.17 us (9%)
  local copies, waits for them, and re-layouts  8.86 us (8%)
  other arithmetic  8.36 us (8%)
  matrix products  7.13 us (7%)
  starting transfers between devices  4.88 us (5%)
  between operations  2.85 us (3%)
    unnamed x1, blocking collectives  35.4 us
    all_gather x1, blocking collectives, local(): group_text = lax.all_gather(text, 'grp', axis=0, tiled=True)  28.1 us
    ppermute x11, waiting for transfers between devices, passed_along(): return lax.ppermute(block, axis, route)  9.17 us
    unnamed x13, local copies, waits for them, and re-layouts  7.48 us
    sub x4, other arithmetic, image_terms(): weights = jax.nn.softmax(scores, axis=-1)  5.22 us
    ppermute x11, starting transfers between devices, passed_along(): return lax.ppermute(block, axis, route)  4.88 us
  transfers between devices with their start and end apart: 11, of which 4 were waited for; matrix products, arithmetic and copies ran while one was open for 20% of the time, Pallas kernels for 0%

commit v1 on v0

v1 whole, which is shorter than its diff:
```python
import functools
import math

import jax
import jax.numpy as jnp
from jax import lax
from jax.experimental import pallas as pl
from jax.experimental.pallas import tpu as pltpu
from jax.sharding import PartitionSpec as P

HEADS = 8
EPS = 1e-06
LOGIT_SCALE = 10.0
LOGIT_BIAS = -1.0
LANES = 128
CHUNK = 32
MESH = pl.DeviceIdType.MESH
LAST = (((1,), (1,)), ((), ()))
FIRST = (((0,), (0,)), ((), ()))


def matmul(a, b, dims=None):
    if dims is None:
        return jnp.dot(a, b, preferred_element_type=jnp.float32)
    return lax.dot_general(a, b, dims, preferred_element_type=jnp.float32)


def kernel(
    groups, members,
    text_hbm, keys_hbm, values_hbm, pair_hbm,
    loss_out, text_out, keys_out, values_out,
    text_own, text_all, keys, values, pairs, part, landed,
    in_sem, pair_sem, gather_send, gather_recv, part_send, part_recv,
):
    n = groups * members
    width = keys.shape[1]
    tiles = width // LANES
    depth = width // HEADS
    me = lax.axis_index("blk") * members + lax.axis_index("grp")

    def device(i):
        return (i // members, lax.rem(i, members))

    text_in = pltpu.make_async_copy(text_hbm, text_own, in_sem.at[0])
    keys_in = pltpu.make_async_copy(keys_hbm.at[0], keys, in_sem.at[1])
    values_in = pltpu.make_async_copy(values_hbm.at[0], values, in_sem.at[2])
    pair_in = pltpu.make_async_copy(pair_hbm, pairs, pair_sem)
    text_in.start()
    barrier = pltpu.get_barrier_semaphore()

    def greet(k, _):
        pl.semaphore_signal(
            barrier, inc=1, device_id=device(lax.rem(me + k, n)), device_id_type=MESH
        )
        return 0

    lax.fori_loop(1, n, greet, 0)
    pair_in.start()
    keys_in.start()
    values_in.start()
    text_in.wait()
    own = text_own[...].astype(jnp.float32)
    for j in range(tiles):
        text_all[me, j : j + 1, :] = own[:, j * LANES : (j + 1) * LANES]
    pl.semaphore_wait(barrier, n - 1)

    def spread(k, _):
        pltpu.make_async_remote_copy(
            src_ref=text_all.at[me],
            dst_ref=text_all.at[me],
            send_sem=gather_send,
            recv_sem=gather_recv,
            device_id=device(lax.rem(me + k, n)),
            device_id_type=MESH,
        ).start()
        return 0

    lax.fori_loop(1, n, spread, 0)
    pair_in.wait()
    keys_in.wait()
    values_in.wait()

    def all_of(ref, sem):
        some = ref.at[pl.ds(0, n - 1)]
        pltpu.make_async_copy(some, some, sem).wait()

    count = min(CHUNK, n)
    chunks = n // count
    low_one = lax.broadcasted_iota(jnp.int32, (count, LANES), 1) < depth
    rows = lax.broadcasted_iota(jnp.int32, (count, 1), 0)

    def halves(x):
        zero = jnp.zeros_like(x)
        return jnp.concatenate(
            [jnp.where(low_one, x, zero), jnp.where(low_one, zero, x)], axis=0
        ).astype(jnp.bfloat16)

    def joined(x):
        return jnp.where(low_one, x[:count], x[count:])

    def total(terms):
        return jnp.sum(functools.reduce(lambda a, b: a + b, terms), axis=1, keepdims=True)

    def mine_of(base):
        def look(i, found):
            return jnp.where(rows == i, pairs[base + i], found)

        found = lax.fori_loop(0, count, look, jnp.zeros((count, 1), jnp.int32))
        return jnp.where(found == me, 1.0, -1.0).astype(jnp.float32)

    def tile(ref, j):
        return ref[:, j * LANES : (j + 1) * LANES]

    def one_chunk(base, label, first):
        text = [text_all[pl.ds(base, count), j, :] for j in range(tiles)]
        tnorm = lax.rsqrt(total([t * t for t in text]) / width + EPS)
        normed = [t * tnorm for t in text]
        queries = [halves(t) for t in text]
        weights, attn, pooled = [], [], []
        for j in range(tiles):
            scores = matmul(queries[j], tile(keys, j), LAST)
            top = jnp.max(scores, axis=1, keepdims=True)
            raised = jnp.exp2((scores - top) * (depth ** (-0.5) * math.log2(math.e)))
            weight = raised * (1.0 / jnp.sum(raised, axis=1, keepdims=True))
            weights.append(weight)
            attn.append(weight.astype(jnp.bfloat16))
            pooled.append(joined(matmul(attn[j], tile(values, j))))
        pnorm = lax.rsqrt(total([p * p for p in pooled]) / width + EPS)
        cosine = pnorm * (total([p * t for p, t in zip(pooled, normed)]) / width)
        unit = [p * pnorm for p in pooled]
        logit = LOGIT_SCALE * cosine + LOGIT_BIAS
        z = -label * logit
        loss = jnp.maximum(z, 0.0) + jnp.log1p(jnp.exp(-jnp.abs(z)))
        dcos = LOGIT_SCALE / width * (-label / (1.0 + jnp.exp(-z)))
        into = pnorm * dcos
        back = tnorm * dcos
        dout, dscore = [], []
        for j in range(tiles):
            dout.append(halves(into * (normed[j] - unit[j] * cosine)))
            dattn = matmul(dout[j], tile(values, j), LAST)
            level = jnp.sum(weights[j] * dattn, axis=1, keepdims=True)
            dscore.append(
                (weights[j] * (dattn - level) * depth ** (-0.5)).astype(jnp.bfloat16)
            )
            grad = joined(matmul(dscore[j], tile(keys, j)))
            part[pl.ds(base, count), j, :] = grad + back * (unit[j] - normed[j] * cosine)
        part[pl.ds(base, count), tiles, :] = jnp.broadcast_to(loss, (count, LANES))

        def deliver(k, _):
            to = base + lax.rem(me + k, count)

            @pl.when(to != me)
            def _():
                pltpu.make_async_remote_copy(
                    src_ref=part.at[to],
                    dst_ref=landed.at[me],
                    send_sem=part_send,
                    recv_sem=part_recv,
                    device_id=device(to),
                    device_id_type=MESH,
                ).start()

            return 0

        lax.fori_loop(0, count, deliver, 0)
        for j in range(tiles):
            lanes = pl.ds(j * LANES, LANES)
            gk = matmul(dscore[j], queries[j], FIRST)
            gv = matmul(attn[j], dout[j], FIRST)
            if first:
                keys_out[0, :, lanes] = gk
                values_out[0, :, lanes] = gv
            else:
                keys_out[0, :, lanes] += gk
                values_out[0, :, lanes] += gv

    if chunks == 1:
        label = mine_of(0)
        all_of(text_all, gather_recv)
        one_chunk(0, label, True)
    else:
        all_of(text_all, gather_recv)
        keys_out[...] = jnp.zeros_like(keys_out)
        values_out[...] = jnp.zeros_like(values_out)

        def body(c, _):
            base = pl.multiple_of(c * count, count)
            one_chunk(base, mine_of(base), False)
            return 0

        lax.fori_loop(0, chunks, body, 0)
    landed[me] = part[me]
    all_of(part, part_recv)
    if chunks == 1:
        got = functools.reduce(lambda a, b: a + b, [landed[i] for i in range(n)])
    else:
        got = lax.fori_loop(
            0, n, lambda i, a: a + landed[i], jnp.zeros(landed.shape[1:], jnp.float32)
        )
    for j in range(tiles):
        text_out[:, j * LANES : (j + 1) * LANES] = got[j : j + 1]
    loss_out[...] = got[tiles : tiles + 1, 0:1] / n
    all_of(text_all, gather_send)
    all_of(part, part_send)


def local(groups, members, text, keys, values, pair_image):
    n = groups * members
    patches, width = keys.shape[1:]
    tiles = width // LANES
    anywhere = pl.BlockSpec(memory_space=pl.ANY)
    vmem = pl.BlockSpec(memory_space=pltpu.VMEM)
    loss, grad_text, grad_keys, grad_values = pl.pallas_call(
        functools.partial(kernel, groups, members),
        out_shape=(
            jax.ShapeDtypeStruct((1, 1), jnp.float32),
            jax.ShapeDtypeStruct(text.shape, jnp.float32),
            jax.ShapeDtypeStruct(keys.shape, jnp.float32),
            jax.ShapeDtypeStruct(values.shape, jnp.float32),
        ),
        in_specs=[anywhere] * 4,
        out_specs=(vmem, vmem, vmem, vmem),
        scratch_shapes=[
            pltpu.VMEM(text.shape, jnp.bfloat16),
            pltpu.VMEM((n, tiles, LANES), jnp.float32),
            pltpu.VMEM((patches, width), jnp.bfloat16),
            pltpu.VMEM((patches, width), jnp.bfloat16),
            pltpu.SMEM((n,), jnp.int32),
            pltpu.VMEM((n, tiles + 1, LANES), jnp.float32),
            pltpu.VMEM((n, tiles + 1, LANES), jnp.float32),
            pltpu.SemaphoreType.DMA((3,)),
            pltpu.SemaphoreType.DMA,
            pltpu.SemaphoreType.DMA,
            pltpu.SemaphoreType.DMA,
            pltpu.SemaphoreType.DMA,
            pltpu.SemaphoreType.DMA,
        ],
        compiler_params=pltpu.CompilerParams(collective_id=0, has_side_effects=True),
        name="pool",
    )(text, keys, values, pair_image)
    return loss.reshape(1), grad_text, grad_keys, grad_values


def solution(mesh):
    groups, members = mesh.shape["blk"], mesh.shape["grp"]
    both = ("blk", "grp")
    placed = (P(both, None), P(both, None, None), P(both, None, None), P())
    return jax.shard_map(
        functools.partial(local, groups, members),
        mesh=mesh,
        in_specs=placed,
        out_specs=(P(both), P(both, None), P(both, None, None), P(both, None, None)),
        check_vma=False,
    )
```

time: 105 us -> 27 us (0.26)
  blocking collectives: 63.5 us -> 0 us
  Pallas kernels: 0 us -> 20.6 us
  waiting for transfers between devices: 9.17 us -> 0 us
  other arithmetic: 8.36 us -> 0 us
  matrix products: 7.13 us -> 0 us
  local copies, waits for them, and re-layouts: 8.86 us -> 3.96 us
  starting transfers between devices: 4.88 us -> 0 us
    unnamed x1 -> x0, blocking collectives: 35.4 us -> none
    all_gather x1 -> x0, blocking collectives: 28.1 us -> none  [local(): group_text = lax.all_gather(text, 'grp', axis=0, tiled=True)]
    pallas_call x0 -> x1, Pallas kernels: none -> 20.6 us  [local(): pl.pallas_call(functools.partial(kernel, groups, members), out_shape=(jax...]
    ppermute x11 -> x0, waiting for transfers between devices: 9.17 us -> none  [passed_along(): return lax.ppermute(block, axis, route)]
    dot_general x24 -> x0, matrix products: 7.13 us -> none  [the longest x4 1.73 us: image_terms(): jnp.einsum('chp,chd->phd', dscore, queries, preferred_element_type=jnp.fl...]
    sub x4 -> x0, other arithmetic: 5.22 us -> none  [image_terms(): weights = jax.nn.softmax(scores, axis=-1)]
    ppermute x11 -> x0, starting transfers between devices: 4.88 us -> none  [passed_along(): return lax.ppermute(block, axis, route)]
    unnamed x13 -> x7, local copies, waits for them, and re-layouts: 7.48 us -> 3.96 us
  transfers between devices with their start and end apart: 11 -> 0, of which waited for: 4 -> 0; matrix products, arithmetic and copies ran while one was open for 20% -> 0% of each run, Pallas kernels for 0% -> 0%
where the time goes in v1:
time: 27 us; the launch traced here: 26.9 us
  Pallas kernels  20.6 us (76%)
  local copies, waits for them, and re-layouts  3.96 us (15%)
  between operations  2.35 us (9%)
    pallas_call x1, Pallas kernels, local(): pl.pallas_call(functools.partial(kernel, groups, members), out_shape=(jax...  20.6 us
    unnamed x7, local copies, waits for them, and re-layouts  3.96 us

profile of v1, /device:TPU:0, one launch (start us, length us, event | category | flops | bytes accessed | tf_op | source)
XLA Modules:
  0.0 26.9 jit_solution(7146495018202013785)
XLA Ops:
  0.6 20.6 %pool.1 = (f32[1,1]{1,0:T(1,128)}, f32[1,512]{1,0:T(1,128)}, f32[1,196,512]{2,1,0:T(8,128)}, f32[1,196,512]{2,1,0:T(8,128)}) custom-call(bf16[1,512]{1,0:T(2,128)(2,1)} %text_hbm.1, bf16[1,196,512]{2,1,0:T(8,128)(2,1)} %keys_hbm.1, bf16[1,196,512]{2,1,0:T(8,128)(2,1)} %values_hbm.1, s32[32]{0:T(128)} %pair_hbm.1), custom_call_target="tpu_custom_call" | custom-call | tf_op jit(solution)/shard_map/pool/pallas_call | solution.py:213
  21.2 0.0 copy-start
  21.2 2.2 %copy.8 = f32[1,196,512]{2,0,1:T(1,128)} copy(f32[1,196,512]{2,1,0:T(8,128)} %get-tuple-element.14) | data formatting | bytes 802816
  23.4 0.0 copy-done
  23.4 0.0 copy-start.1
  23.4 1.2 %copy.9 = f32[1,196,512]{2,0,1:T(1,128)} copy(f32[1,196,512]{2,1,0:T(8,128)S(1)} %copy-done) | data formatting | bytes 802816
  25.1 0.0 copy-done.1
  25.2 0.6 %copy.13 = f32[1,512]{1,0:T(1,128)} copy(f32[1,512]{1,0:T(1,128)S(1)} %copy-done.1) | data formatting | bytes 4096
Async XLA Ops:
  21.2 2.2 %copy-start = (f32[1,196,512]{2,1,0:T(8,128)S(1)}, f32[1,196,512]{2,1,0:T(8,128)}, u32[]{:S(2)}) copy-start(f32[1,196,512]{2,1,0:T(8,128)} %get-tuple-element.15) | copy-start | bytes 1204228
  23.4 1.7 %copy-start.1 = (f32[1,512]{1,0:T(1,128)S(1)}, f32[1,512]{1,0:T(1,128)}, u32[]{:S(2)}) copy-start(f32[1,512]{1,0:T(1,128)} %get-tuple-element.21) | copy-start | bytes 6148

commit v2 on v1

--- a/solution.py
+++ b/solution.py
@@ -14,7 +14,7 @@
 LOGIT_BIAS = -1.0
 LANES = 128
 CHUNK = 32
-MESH = pl.DeviceIdType.MESH
+LOGICAL = pl.DeviceIdType.LOGICAL
 LAST = (((1,), (1,)), ((), ()))
 FIRST = (((0,), (0,)), ((), ()))
 
@@ -29,7 +29,7 @@
     groups, members,
     text_hbm, keys_hbm, values_hbm, pair_hbm,
     loss_out, text_out, keys_out, values_out,
-    text_own, text_all, keys, values, pairs, part, landed,
+    text_own, text_all, wide, keys, values, pairs, part, landed,
     in_sem, pair_sem, gather_send, gather_recv, part_send, part_recv,
 ):
     n = groups * members
@@ -38,8 +38,21 @@
     depth = width // HEADS
     me = lax.axis_index("blk") * members + lax.axis_index("grp")
 
-    def device(i):
-        return (i // members, lax.rem(i, members))
+    def peer(k):
+        other = me + k
+        return jnp.where(other >= n, other - n, other)
+
+    def each(low, high, step):
+        if high - low <= CHUNK:
+            for k in range(low, high):
+                step(k)
+        else:
+
+            def body(k, _):
+                step(k)
+                return 0
+
+            lax.fori_loop(low, high, body, 0)
 
     text_in = pltpu.make_async_copy(text_hbm, text_own, in_sem.at[0])
     keys_in = pltpu.make_async_copy(keys_hbm.at[0], keys, in_sem.at[1])
@@ -48,34 +61,31 @@
     text_in.start()
     barrier = pltpu.get_barrier_semaphore()
 
-    def greet(k, _):
-        pl.semaphore_signal(
-            barrier, inc=1, device_id=device(lax.rem(me + k, n)), device_id_type=MESH
-        )
-        return 0
-
-    lax.fori_loop(1, n, greet, 0)
+    def greet(k):
+        pl.semaphore_signal(barrier, inc=1, device_id=peer(k), device_id_type=LOGICAL)
+
+    each(1, n, greet)
     pair_in.start()
     keys_in.start()
     values_in.start()
     text_in.wait()
     own = text_own[...].astype(jnp.float32)
-    for j in range(tiles):
-        text_all[me, j : j + 1, :] = own[:, j * LANES : (j + 1) * LANES]
+    text_all[me] = jnp.concatenate(
+        [own[:, j * LANES : (j + 1) * LANES] for j in range(tiles)], axis=0
+    ).astype(jnp.bfloat16)
     pl.semaphore_wait(barrier, n - 1)
 
-    def spread(k, _):
+    def spread(k):
         pltpu.make_async_remote_copy(
             src_ref=text_all.at[me],
             dst_ref=text_all.at[me],
             send_sem=gather_send,
             recv_sem=gather_recv,
-            device_id=device(lax.rem(me + k, n)),
-            device_id_type=MESH,
+            device_id=peer(k),
+            device_id_type=LOGICAL,
         ).start()
-        return 0
-
-    lax.fori_loop(1, n, spread, 0)
+
+    each(1, n, spread)
     pair_in.wait()
     keys_in.wait()
     values_in.wait()
@@ -102,17 +112,17 @@
         return jnp.sum(functools.reduce(lambda a, b: a + b, terms), axis=1, keepdims=True)
 
     def mine_of(base):
-        def look(i, found):
-            return jnp.where(rows == i, pairs[base + i], found)
-
-        found = lax.fori_loop(0, count, look, jnp.zeros((count, 1), jnp.int32))
+        found = jnp.zeros((count, 1), jnp.int32)
+        for i in range(count):
+            found = jnp.where(rows == i, pairs[base + i], found)
         return jnp.where(found == me, 1.0, -1.0).astype(jnp.float32)
 
     def tile(ref, j):
         return ref[:, j * LANES : (j + 1) * LANES]
 
     def one_chunk(base, label, first):
-        text = [text_all[pl.ds(base, count), j, :] for j in range(tiles)]
+        wide[...] = text_all[pl.ds(base, count)].astype(jnp.float32)
+        text = [wide[:, j, :] for j in range(tiles)]
         tnorm = lax.rsqrt(total([t * t for t in text]) / width + EPS)
         normed = [t * tnorm for t in text]
         queries = [halves(t) for t in text]
@@ -146,33 +156,30 @@
             part[pl.ds(base, count), j, :] = grad + back * (unit[j] - normed[j] * cosine)
         part[pl.ds(base, count), tiles, :] = jnp.broadcast_to(loss, (count, LANES))
 
-        def deliver(k, _):
-            to = base + lax.rem(me + k, count)
-
-            @pl.when(to != me)
-            def _():
-                pltpu.make_async_remote_copy(
-                    src_ref=part.at[to],
-                    dst_ref=landed.at[me],
-                    send_sem=part_send,
-                    recv_sem=part_recv,
-                    device_id=device(to),
-                    device_id_type=MESH,
-                ).start()
-
-            return 0
-
-        lax.fori_loop(0, count, deliver, 0)
+        def deliver(to):
+            pltpu.make_async_remote_copy(
+                src_ref=part.at[to],
+                dst_ref=landed.at[me],
+                send_sem=part_send,
+                recv_sem=part_recv,
+                device_id=to,
+                device_id_type=LOGICAL,
+            ).start()
+
+        if first:
+            each(1, n, lambda k: deliver(peer(k)))
+        else:
+            each(0, count, lambda k: pl.when(base + k != me)(lambda: deliver(base + k)))
         for j in range(tiles):
-            lanes = pl.ds(j * LANES, LANES)
+            lanes = pl.ds(j, keys.shape[0], stride=tiles)
             gk = matmul(dscore[j], queries[j], FIRST)
             gv = matmul(attn[j], dout[j], FIRST)
             if first:
-                keys_out[0, :, lanes] = gk
-                values_out[0, :, lanes] = gv
+                keys_out[lanes, :] = gk
+                values_out[lanes, :] = gv
             else:
-                keys_out[0, :, lanes] += gk
-                values_out[0, :, lanes] += gv
+                keys_out[lanes, :] += gk
+                values_out[lanes, :] += gv
 
     if chunks == 1:
         label = mine_of(0)
@@ -213,16 +220,17 @@
     loss, grad_text, grad_keys, grad_values = pl.pallas_call(
         functools.partial(kernel, groups, members),
         out_shape=(
-            jax.ShapeDtypeStruct((1, 1), jnp.float32),
-            jax.ShapeDtypeStruct(text.shape, jnp.float32),
-            jax.ShapeDtypeStruct(keys.shape, jnp.float32),
-            jax.ShapeDtypeStruct(values.shape, jnp.float32),
+            pltpu.VMEM((1, 1), jnp.float32),
+            pltpu.VMEM(text.shape, jnp.float32),
+            pltpu.VMEM((patches * tiles, LANES), jnp.float32),
+            pltpu.VMEM((patches * tiles, LANES), jnp.float32),
         ),
         in_specs=[anywhere] * 4,
         out_specs=(vmem, vmem, vmem, vmem),
         scratch_shapes=[
             pltpu.VMEM(text.shape, jnp.bfloat16),
-            pltpu.VMEM((n, tiles, LANES), jnp.float32),
+            pltpu.VMEM((n, tiles, LANES), jnp.bfloat16),
+            pltpu.VMEM((min(CHUNK, n), tiles, LANES), jnp.float32),
             pltpu.VMEM((patches, width), jnp.bfloat16),
             pltpu.VMEM((patches, width), jnp.bfloat16),
             pltpu.SMEM((n,), jnp.int32),
@@ -238,7 +246,12 @@
         compiler_params=pltpu.CompilerParams(collective_id=0, has_side_effects=True),
         name="pool",
     )(text, keys, values, pair_image)
-    return loss.reshape(1), grad_text, grad_keys, grad_values
+    return (
+        loss.reshape(1),
+        grad_text,
+        grad_keys.reshape(keys.shape),
+        grad_values.reshape(values.shape),
+    )
 
 
 def solution(mesh):

time: 27 us -> 23.2 us (0.86)
  local copies, waits for them, and re-layouts: 3.96 us -> 2.08 us
  Pallas kernels: 20.6 us -> 19.2 us
  between operations: 2.35 us -> 1.8 us
    unnamed x7 -> x3, local copies, waits for them, and re-layouts: 3.96 us -> 2.08 us
    pallas_call x1, Pallas kernels: 20.6 us -> 19.2 us  [local(): pl.pallas_call(functools.partial(kernel, groups, members), out_shape=(plt...]
where the time goes in v2:
time: 23.2 us; the launch traced here: 23.1 us
  Pallas kernels  19.2 us (83%)
  local copies, waits for them, and re-layouts  2.08 us (9%)
  between operations  1.8 us (8%)
    pallas_call x1, Pallas kernels, local(): pl.pallas_call(functools.partial(kernel, groups, members), out_shape=(plt...  19.2 us
    unnamed x3, local copies, waits for them, and re-layouts  2.08 us

profile of v2, /device:TPU:0, one launch (start us, length us, event | category | flops | bytes accessed | tf_op | source)
XLA Modules:
  0.0 23.1 jit_solution(9456312442647080509)
XLA Ops:
  0.6 19.2 %pool.1 = (f32[1,1]{1,0:T(1,128)S(1)}, f32[1,512]{1,0:T(1,128)S(1)}, f32[784,128]{1,0:T(8,128)S(1)}, f32[784,128]{1,0:T(8,128)S(1)}) custom-call(bf16[1,512]{1,0:T(2,128)(2,1)} %text_hbm.1, bf16[1,196,512]{2,1,0:T(8,128)(2,1)} %keys_hbm.1, bf16[1,196,512]{2,1,0:T(8,128)(2,1)} %values_hbm.1, s32[32]{0:T(128)} %pair_hbm.1), custom_call_target="tpu_custom_call" | custom-call | tf_op jit(solution)/shard_map/pool/pallas_call | solution.py:220
  19.9 0.6 %copy.17 = f32[1,512]{1,0:T(1,128)} copy(f32[1,512]{1,0:T(1,128)S(1)} %get-tuple-element.21) | data formatting | bytes 4096
  20.5 0.7 %copy.18 = f32[1,196,512]{2,0,1:T(1,128)} copy(f32[1,196,512]{2,0,1:T(1,128)S(1)} %bitcast.4) | data formatting | bytes 802816
  21.2 0.7 %copy.19 = f32[1,196,512]{2,0,1:T(1,128)} copy(f32[1,196,512]{2,0,1:T(1,128)S(1)} %bitcast.3) | data formatting | bytes 802816

commit v3 on v2

--- a/solution.py
+++ b/solution.py
@@ -211,13 +211,25 @@
     all_of(part, part_send)
 
 
+def store(*refs):
+    sources, targets, sem = refs[:4], refs[4:8], refs[8]
+    copies = [
+        pltpu.make_async_copy(source, target, sem.at[i])
+        for i, (source, target) in enumerate(zip(sources, targets))
+    ]
+    for copy in copies:
+        copy.start()
+    for copy in copies:
+        copy.wait()
+
+
 def local(groups, members, text, keys, values, pair_image):
     n = groups * members
     patches, width = keys.shape[1:]
     tiles = width // LANES
     anywhere = pl.BlockSpec(memory_space=pl.ANY)
     vmem = pl.BlockSpec(memory_space=pltpu.VMEM)
-    loss, grad_text, grad_keys, grad_values = pl.pallas_call(
+    results = pl.pallas_call(
         functools.partial(kernel, groups, members),
         out_shape=(
             pltpu.VMEM((1, 1), jnp.float32),
@@ -246,6 +258,15 @@
         compiler_params=pltpu.CompilerParams(collective_id=0, has_side_effects=True),
         name="pool",
     )(text, keys, values, pair_image)
+    results = [pltpu.with_memory_space_constraint(r, pltpu.VMEM) for r in results]
+    loss, grad_text, grad_keys, grad_values = pl.pallas_call(
+        store,
+        out_shape=[jax.ShapeDtypeStruct(r.shape, r.dtype) for r in results],
+        in_specs=[vmem] * 4,
+        out_specs=[anywhere] * 4,
+        scratch_shapes=[pltpu.SemaphoreType.DMA((4,))],
+        name="store",
+    )(*results)
     return (
         loss.reshape(1),
         grad_text,

time: 23.2 us -> 22.1 us (0.953)
  Pallas kernels: 19.2 us -> 21.3 us
  local copies, waits for them, and re-layouts: 2.08 us -> 0 us
  between operations: 1.8 us -> 0.64 us
    unnamed x3 -> x0, local copies, waits for them, and re-layouts: 2.08 us -> none
    pallas_call x0 -> x1, Pallas kernels: none -> 1.56 us  [local(): pl.pallas_call(store, out_shape=[jax.ShapeDtypeStruct(r.shape, r.dtype) f...]
    pallas_call x1, Pallas kernels: 19.2 us -> 19.7 us  [local(): pl.pallas_call(functools.partial(kernel, groups, members), out_shape=(plt...]
where the time goes in v3:
time: 22.1 us; the launch traced here: 21.9 us
  Pallas kernels  21.3 us (96%)
  between operations  0.64 us (3%)
    pallas_call x1, Pallas kernels, local(): pl.pallas_call(functools.partial(kernel, groups, members), out_shape=(plt...  19.7 us
    pallas_call x1, Pallas kernels, local(): pl.pallas_call(store, out_shape=[jax.ShapeDtypeStruct(r.shape, r.dtype) f...  1.56 us

profile of v3, /device:TPU:0, one launch (start us, length us, event | category | flops | bytes accessed | tf_op | source)
XLA Modules:
  0.0 21.9 jit_solution(3305702495486057160)
XLA Ops:
  0.6 19.7 %pool.1 = (f32[1,1]{1,0:T(1,128)}, f32[1,512]{1,0:T(1,128)S(1)}, f32[784,128]{1,0:T(8,128)S(1)}, f32[784,128]{1,0:T(8,128)S(1)}) custom-call(bf16[1,512]{1,0:T(2,128)(2,1)} %text_hbm.1, bf16[1,196,512]{2,1,0:T(8,128)(2,1)} %keys_hbm.1, bf16[1,196,512]{2,1,0:T(8,128)(2,1)} %values_hbm.1, s32[32]{0:T(128)} %pair_hbm.1), custom_call_target="tpu_custom_call" | custom-call | tf_op jit(solution)/shard_map/pool/pallas_call | solution.py:232
  20.4 1.6 %store.1 = (f32[1,1]{1,0:T(1,128)}, f32[1,512]{1,0:T(1,128)}, f32[784,128]{1,0:T(8,128)}, f32[784,128]{1,0:T(8,128)}) custom-call(f32[1,1]{1,0:T(1,128)} %get-tuple-element.12.refs_0_, f32[1,512]{1,0:T(1,128)S(1)} %get-tuple-element.13.refs_1_, f32[784,128]{1,0:T(8,128)S(1)} %get-tuple-element.14.refs_2_, f32[784,128]{1,0:T(8,128)S(1)} %get-tuple-element.15.refs_3_), custom_call_target="tpu_custom_call" | custom-call | tf_op jit(solution)/shard_map/store/pallas_call | solution.py:262

commit v4 on v3

--- a/solution.py
+++ b/solution.py
@@ -126,15 +126,15 @@
         tnorm = lax.rsqrt(total([t * t for t in text]) / width + EPS)
         normed = [t * tnorm for t in text]
         queries = [halves(t) for t in text]
-        weights, attn, pooled = [], [], []
-        for j in range(tiles):
-            scores = matmul(queries[j], tile(keys, j), LAST)
-            top = jnp.max(scores, axis=1, keepdims=True)
-            raised = jnp.exp2((scores - top) * (depth ** (-0.5) * math.log2(math.e)))
-            weight = raised * (1.0 / jnp.sum(raised, axis=1, keepdims=True))
-            weights.append(weight)
-            attn.append(weight.astype(jnp.bfloat16))
-            pooled.append(joined(matmul(attn[j], tile(values, j))))
+        every = range(tiles)
+        scores = [matmul(queries[j], tile(keys, j), LAST) for j in every]
+        tops = [jnp.max(x, axis=1, keepdims=True) for x in scores]
+        rate = depth ** (-0.5) * math.log2(math.e)
+        raised = [jnp.exp2((x - top) * rate) for x, top in zip(scores, tops)]
+        sums = [jnp.sum(x, axis=1, keepdims=True) for x in raised]
+        weights = [x * (1.0 / y) for x, y in zip(raised, sums)]
+        attn = [x.astype(jnp.bfloat16) for x in weights]
+        pooled = [joined(matmul(attn[j], tile(values, j))) for j in every]
         pnorm = lax.rsqrt(total([p * p for p in pooled]) / width + EPS)
         cosine = pnorm * (total([p * t for p, t in zip(pooled, normed)]) / width)
         unit = [p * pnorm for p in pooled]
@@ -144,16 +144,16 @@
         dcos = LOGIT_SCALE / width * (-label / (1.0 + jnp.exp(-z)))
         into = pnorm * dcos
         back = tnorm * dcos
-        dout, dscore = [], []
-        for j in range(tiles):
-            dout.append(halves(into * (normed[j] - unit[j] * cosine)))
-            dattn = matmul(dout[j], tile(values, j), LAST)
-            level = jnp.sum(weights[j] * dattn, axis=1, keepdims=True)
-            dscore.append(
-                (weights[j] * (dattn - level) * depth ** (-0.5)).astype(jnp.bfloat16)
-            )
-            grad = joined(matmul(dscore[j], tile(keys, j)))
-            part[pl.ds(base, count), j, :] = grad + back * (unit[j] - normed[j] * cosine)
+        dout = [halves(into * (normed[j] - unit[j] * cosine)) for j in every]
+        dattn = [matmul(dout[j], tile(values, j), LAST) for j in every]
+        levels = [jnp.sum(weights[j] * dattn[j], axis=1, keepdims=True) for j in every]
+        dscore = [
+            (weights[j] * (dattn[j] - levels[j]) * depth ** (-0.5)).astype(jnp.bfloat16)
+            for j in every
+        ]
+        grads = [joined(matmul(dscore[j], tile(keys, j))) for j in every]
+        for j in every:
+            part[pl.ds(base, count), j, :] = grads[j] + back * (unit[j] - normed[j] * cosine)
         part[pl.ds(base, count), tiles, :] = jnp.broadcast_to(loss, (count, LANES))
 
         def deliver(to):

time: 22.1 us -> 20.4 us (0.923)
  Pallas kernels: 21.3 us -> 19.5 us
    pallas_call x1, Pallas kernels: 19.7 us -> 18 us  [local(): pl.pallas_call(functools.partial(kernel, groups, members), out_shape=(plt...]
where the time goes in v4:
time: 20.4 us; the launch traced here: 20.2 us
  Pallas kernels  19.5 us (96%)
  between operations  0.64 us (3%)
    pallas_call x1, Pallas kernels, local(): pl.pallas_call(functools.partial(kernel, groups, members), out_shape=(plt...  18 us
    pallas_call x1, Pallas kernels, local(): pl.pallas_call(store, out_shape=[jax.ShapeDtypeStruct(r.shape, r.dtype) f...  1.56 us

profile of v4, /device:TPU:0, one launch (start us, length us, event | category | flops | bytes accessed | tf_op | source)
XLA Modules:
  0.0 20.2 jit_solution(14293437106565838921)
XLA Ops:
  0.6 18.0 %pool.1 = (f32[1,1]{1,0:T(1,128)}, f32[1,512]{1,0:T(1,128)S(1)}, f32[784,128]{1,0:T(8,128)S(1)}, f32[784,128]{1,0:T(8,128)S(1)}) custom-call(bf16[1,512]{1,0:T(2,128)(2,1)} %text_hbm.1, bf16[1,196,512]{2,1,0:T(8,128)(2,1)} %keys_hbm.1, bf16[1,196,512]{2,1,0:T(8,128)(2,1)} %values_hbm.1, s32[32]{0:T(128)} %pair_hbm.1), custom_call_target="tpu_custom_call" | custom-call | tf_op jit(solution)/shard_map/pool/pallas_call | solution.py:232
  18.6 1.6 %store.1 = (f32[1,1]{1,0:T(1,128)}, f32[1,512]{1,0:T(1,128)}, f32[784,128]{1,0:T(8,128)}, f32[784,128]{1,0:T(8,128)}) custom-call(f32[1,1]{1,0:T(1,128)} %get-tuple-element.12.refs_0_, f32[1,512]{1,0:T(1,128)S(1)} %get-tuple-element.13.refs_1_, f32[784,128]{1,0:T(8,128)S(1)} %get-tuple-element.14.refs_2_, f32[784,128]{1,0:T(8,128)S(1)} %get-tuple-element.15.refs_3_), custom_call_target="tpu_custom_call" | custom-call | tf_op jit(solution)/shard_map/store/pallas_call | solution.py:262

commit v5 on v4

--- a/solution.py
+++ b/solution.py
@@ -75,17 +75,21 @@
     ).astype(jnp.bfloat16)
     pl.semaphore_wait(barrier, n - 1)
 
-    def spread(k):
+    def spread(to):
         pltpu.make_async_remote_copy(
             src_ref=text_all.at[me],
             dst_ref=text_all.at[me],
             send_sem=gather_send,
             recv_sem=gather_recv,
-            device_id=peer(k),
+            device_id=to,
             device_id_type=LOGICAL,
         ).start()
 
-    each(1, n, spread)
+    if n <= CHUNK:
+        for to in reversed(range(n)):
+            pl.when(to != me)(functools.partial(spread, to))
+    else:
+        each(1, n, lambda k: spread(peer(k)))
     pair_in.wait()
     keys_in.wait()
     values_in.wait()

time: 20.4 us -> 20.2 us (level)
  no operation moved by 1% of the time
where the time goes in v5:
time: 20.2 us; the launch traced here: 20 us
  Pallas kernels  19.3 us (96%)
  between operations  0.64 us (3%)
    pallas_call x1, Pallas kernels, local(): pl.pallas_call(functools.partial(kernel, groups, members), out_shape=(plt...  17.8 us
    pallas_call x1, Pallas kernels, local(): pl.pallas_call(store, out_shape=[jax.ShapeDtypeStruct(r.shape, r.dtype) f...  1.56 us

profile of v5, /device:TPU:0, one launch (start us, length us, event | category | flops | bytes accessed | tf_op | source)
XLA Modules:
  0.0 20.0 jit_solution(7147255552550452395)
XLA Ops:
  0.6 17.8 %pool.1 = (f32[1,1]{1,0:T(1,128)}, f32[1,512]{1,0:T(1,128)S(1)}, f32[784,128]{1,0:T(8,128)S(1)}, f32[784,128]{1,0:T(8,128)S(1)}) custom-call(bf16[1,512]{1,0:T(2,128)(2,1)} %text_hbm.1, bf16[1,196,512]{2,1,0:T(8,128)(2,1)} %keys_hbm.1, bf16[1,196,512]{2,1,0:T(8,128)(2,1)} %values_hbm.1, s32[32]{0:T(128)} %pair_hbm.1), custom_call_target="tpu_custom_call" | custom-call | tf_op jit(solution)/shard_map/pool/pallas_call | solution.py:236
  18.4 1.6 %store.1 = (f32[1,1]{1,0:T(1,128)}, f32[1,512]{1,0:T(1,128)}, f32[784,128]{1,0:T(8,128)}, f32[784,128]{1,0:T(8,128)}) custom-call(f32[1,1]{1,0:T(1,128)} %get-tuple-element.12.refs_0_, f32[1,512]{1,0:T(1,128)S(1)} %get-tuple-element.13.refs_1_, f32[784,128]{1,0:T(8,128)S(1)} %get-tuple-element.14.refs_2_, f32[784,128]{1,0:T(8,128)S(1)} %get-tuple-element.15.refs_3_), custom_call_target="tpu_custom_call" | custom-call | tf_op jit(solution)/shard_map/store/pallas_call | solution.py:266
